TPU v7x, 32 devices: a whole 2x2x4 slice. The times are simulated.
32 devices in a mesh: win: 2 (over y), dx: 4 (over z), dy: 2 (over x), dz: 2 (over core).
Axes of the slice: x: 2, y: 2, z: 4, core: 2. Of those that a mesh axis runs over, the one named last changes fastest.
Arguments:
- fraction: float32 [3, 8, 2, 2, 768], P(None, ('win', 'dx'), 'dy', 'dz'), parts along dimension 1, may hold values from 0 to 1
- atom_type: int32 [8, 2, 2, 768], P(('win', 'dx'), 'dy', 'dz'), parts along dimension 0, may hold values from 0 to 31
- perturbed: int32 [8, 2, 2, 768], P(('win', 'dx'), 'dy', 'dz'), parts along dimension 0, may hold values from 0 to 1
- leaving: int32 [8, 2, 2, 2, 16], P(('win', 'dx'), 'dy', 'dz'), parts along dimension 0, may hold values from 0 to 767, as said below
- neighbours: int32 [8, 2, 2, 6, 16], P(('win', 'dx'), 'dy', 'dz'), parts along dimension 0, may hold values from 0 to 161, as said below
- counts: int32 [8, 2, 2, 6], P(('win', 'dx'), 'dy', 'dz'), parts along dimension 0, may hold values from 1 to 16, as said below
- sigma_table: float32 [32], replicated, may hold values from 0.8 to 1.2
- depth_table: float32 [32], replicated, may hold values from 0.002 to 0.03
- charge_table: float32 [32], replicated, may hold values from -1 to 1
- domain_edge: float32 [3], replicated, may hold values from 1 to 1.12
- coupling: float32 [2], P('win'), parts along dimension 0, may hold values from 0.1 to 0.9
Outputs:
- forces: float32 [3, 8, 2, 2, 768], P(None, ('win', 'dx'), 'dy', 'dz'), parts along dimension 1
- energy: float32 [2], P('win'), parts along dimension 0
- dhdl: float32 [2], P('win'), parts along dimension 0
There are 2 independent parts, one for each index of `win`. A program takes and returns all parts, laid end to end along the dimension named above; an argument that names none is the same for every part. Nothing has to cross between parts.
Inputs may be any that keep to these rules, and one draw needn't show every extreme that they name: `leaving`: each domain lists 2 * 16 distinct slots: the first 16 leave toward the next domain, the last 16 toward the previous one. `neighbours`: each list holds 16 distinct ghost block numbers; entries at or past the block's count are valid numbers and are not used. `counts`: some block lists exactly 16 blocks in every draw.
All inputs are finite; a program needn't handle non-finite values.
Results may differ from a plain program's by a relative error of at most 0.0003.
Values sent between devices are 32-bit elements; how exact they have to be, the bound alone decides.
A program may use at most 64 MiB of HBM per device.

v0:
```python
import jax
import jax.numpy as jnp
from jax import lax
from jax.sharding import PartitionSpec as P

soft_base = 0.3
soft_alpha = 0.5
charge_base = 0.3
charge_alpha = 0.5
coulomb = 0.1


def passed_along(array, axis, by):
    devices = lax.axis_size(axis)
    return lax.ppermute(array, axis, [(i, (i + by) % devices) for i in range(devices)])


def extended(block, sides, width):
    for axis, dim in sides:
        count = lax.axis_size(axis)
        forward = [(i, i + 1) for i in range(count - 1)]
        forward.append((count - 1, 0))
        backward = [(target, source) for source, target in forward]
        low = lax.ppermute(
            lax.slice_in_dim(block, block.shape[dim] - width, None, axis=dim), axis, forward
        )
        high = lax.ppermute(lax.slice_in_dim(block, 0, width, axis=dim), axis, backward)
        block = jnp.concatenate([low, block, high], axis=dim)
    return block


def swapped(block, axis, bit):
    count = lax.axis_size(axis)
    route = []
    for low in range(count):
        high = low | 1 << bit
        if high != low and high < count:
            route += [(low, high), (high, low)]
    return lax.ppermute(block, axis, route)


def lookup(table_row, type_ids):
    onehot = type_ids[None, :] == jnp.arange(table_row.shape[0], dtype=jnp.int32)[:, None]
    return jnp.sum(jnp.where(onehot, table_row[:, None], jnp.float32(0.0)), axis=0)


def pair_block(own_block, other_blocks, live_pairs, coupling_value):
    separation = own_block[0:3][None, :, :, None] - other_blocks[:, 0:3][:, :, None, :]
    radius_sq = jnp.sum(separation * separation, axis=1)
    sigma_pair = 0.5 * (own_block[3][None, :, None] + other_blocks[:, 3][:, None, :])
    depth_pair = jnp.sqrt(own_block[4][None, :, None] * other_blocks[:, 4][:, None, :])
    charges = own_block[5][None, :, None] * other_blocks[:, 5][:, None, :]
    flagged = jnp.maximum(own_block[6][None, :, None], other_blocks[:, 6][:, None, :])
    scaled = coupling_value * flagged
    sigma_two = sigma_pair * sigma_pair
    sigma_six = sigma_two * sigma_two * sigma_two
    soft_six = sigma_six * (soft_base + soft_alpha * scaled) + radius_sq * radius_sq * radius_sq
    soft_two = charge_base + charge_alpha * scaled + radius_sq
    inverse_six = 1.0 / soft_six
    energy_lj = (
        4.0
        * depth_pair
        * (sigma_six * sigma_six * inverse_six * inverse_six - sigma_six * inverse_six)
    )
    grad_six = (
        4.0
        * depth_pair
        * (
            sigma_six * inverse_six * inverse_six
            - 2.0 * sigma_six * sigma_six * inverse_six * inverse_six * inverse_six
        )
    )
    energy_coul = coulomb * charges * lax.rsqrt(soft_two)
    grad_two = -0.5 * energy_coul / soft_two
    weight = 1.0 - scaled
    total_pair = energy_lj + energy_coul
    pair_energy = jnp.sum(weight * total_pair * live_pairs)
    pair_dhdl = jnp.sum(
        flagged
        * (-total_pair + weight * (grad_six * sigma_six * soft_alpha + grad_two * charge_alpha))
        * live_pairs
    )
    force_scale = -weight * (6.0 * radius_sq * radius_sq * grad_six + 2.0 * grad_two) * live_pairs
    forces = jnp.sum(force_scale[:, None] * separation, axis=(0, 3))
    return (forces, pair_energy, pair_dhdl)


def block_terms(ghost_rows, listed_blocks, list_count, block_id, block_total, coupling_value):
    centre = 13 * block_total + block_id
    own_block = lax.dynamic_index_in_dim(ghost_rows, centre, 0, keepdims=False)
    other_blocks = jnp.take(ghost_rows, listed_blocks, axis=0)
    valid_slot = (jnp.arange(listed_blocks.shape[0], dtype=jnp.int32) < list_count).astype(
        jnp.float32
    )
    is_self = (listed_blocks == centre).astype(jnp.float32)[:, None, None] * jnp.eye(
        128, dtype=jnp.float32
    )[None]
    live_pairs = valid_slot[:, None, None] * (1.0 - is_self)
    return pair_block(own_block, other_blocks, live_pairs, coupling_value)


def on_device(
    fraction,
    atom_type,
    perturbed,
    leaving,
    neighbours,
    counts,
    sigma_table,
    depth_table,
    charge_table,
    domain_edge,
    coupling,
):
    atom_count = fraction.shape[-1]
    block_total = atom_count // 128
    spacing = float(atom_count) ** (1.0 / 3.0)
    type_ids = atom_type.reshape(atom_count)
    payload = jnp.concatenate(
        [
            fraction.reshape(3, atom_count),
            lookup(sigma_table, type_ids)[None],
            lookup(depth_table, type_ids)[None],
            lookup(charge_table, type_ids)[None],
            perturbed.reshape(1, atom_count).astype(jnp.float32),
        ],
        axis=0,
    )
    leave_slots = leaving.reshape(2, -1)
    shift_x = jnp.zeros((7, 1), jnp.float32).at[0].set(1.0)
    upward = payload[:, leave_slots[0]]
    downward = payload[:, leave_slots[1]]
    from_below = passed_along(upward, "dx", 1) - shift_x
    from_above = passed_along(downward, "dx", -1) + shift_x
    moved = payload.at[:, leave_slots[1]].set(from_below).at[:, leave_slots[0]].set(from_above)
    domain_block = moved.reshape(7, 1, 1, 1, atom_count)
    ghost_plane = extended(domain_block, (("dx", 1), ("dy", 2)), 1)
    partner = swapped(ghost_plane, "dz", 0)
    ghost_cells = jnp.concatenate([partner, ghost_plane, partner], axis=3)
    image_steps = jnp.arange(3, dtype=jnp.float32) - 1.0
    position = jnp.stack(
        [
            (ghost_cells[0] + image_steps[:, None, None, None]) * domain_edge[0] * spacing,
            (ghost_cells[1] + image_steps[None, :, None, None]) * domain_edge[1] * spacing,
            (ghost_cells[2] + image_steps[None, None, :, None]) * domain_edge[2] * spacing,
        ],
        axis=0,
    )
    ghost_all = jnp.concatenate([position, ghost_cells[3:]], axis=0)
    ghost_rows = (
        ghost_all.reshape(7, 27, block_total, 128)
        .transpose(1, 2, 0, 3)
        .reshape(27 * block_total, 7, 128)
    )
    listed = neighbours.reshape(block_total, -1)
    listed_count = counts.reshape(block_total)
    coupling_value = coupling[0]

    def one_block(block_id):
        return block_terms(
            ghost_rows,
            listed[block_id],
            listed_count[block_id],
            block_id,
            block_total,
            coupling_value,
        )

    forces, energies, dhdls = lax.map(one_block, jnp.arange(block_total, dtype=jnp.int32))
    forces = forces.transpose(1, 0, 2).reshape(3, 1, 1, 1, atom_count)
    window_energy, window_dhdl = lax.psum((jnp.sum(energies), jnp.sum(dhdls)), ("dx", "dy", "dz"))
    slot_total = jnp.float32(
        atom_count * lax.axis_size("dx") * lax.axis_size("dy") * lax.axis_size("dz")
    )
    energy = (0.5 * window_energy / slot_total).reshape(1)
    dhdl = (0.5 * window_dhdl / slot_total).reshape(1)
    return (forces, energy, dhdl)


def solution(mesh):
    return jax.shard_map(
        on_device,
        mesh=mesh,
        in_specs=(
            P(None, ("win", "dx"), "dy", "dz", None),
            P(("win", "dx"), "dy", "dz", None),
            P(("win", "dx"), "dy", "dz", None),
            P(("win", "dx"), "dy", "dz", None, None),
            P(("win", "dx"), "dy", "dz", None, None),
            P(("win", "dx"), "dy", "dz", None),
            P(),
            P(),
            P(),
            P(),
            P("win"),
        ),
        out_specs=(P(None, ("win", "dx"), "dy", "dz", None), P("win"), P("win")),
        check_vma=False,
    )
```

profile of v0, /device:TPU:0, one launch (start us, length us, event | category | flops | bytes accessed | tf_op | source)
XLA Modules:
  0.0 154.2 jit_solution(11909424343959024680)
XLA Ops:
  2.8 0.8 select_reduce_fusion
  5.1 3.1 %collective-permute-start = (f32[7,16]{0,1:T(8,128)S(1)}, f32[7,16]{0,1:T(8,128)S(1)}, u32[]{:S(2)}, u32[]{:S(2)}) collective-permute-start(f32[7,16]{0,1:T(8,128)S(1)} %bitcast.113), channel_id=1, source_target_pairs={{0,4},{4,8},{8,12},{12,0},{1,5},{5,9},{9,13},{13,1},{2,6},{6,10},{... | collective-permute-start | bytes 1352 | tf_op jit(solution)/shard_map/ppermute | solution.py:15
  8.8 2.1 %collective-permute-start.1 = (f32[7,16]{0,1:T(8,128)S(1)}, f32[7,16]{0,1:T(8,128)S(1)}, u32[]{:S(2)}, u32[]{:S(2)}) collective-permute-start(f32[7,16]{0,1:T(8,128)S(1)} %bitcast.112), channel_id=1, source_target_pairs={{0,12},{4,0},{8,4},{12,8},{1,13},{5,1},{9,5},{13,9},{2,14},{6,2},{... | collective-permute-start | bytes 1352 | tf_op jit(solution)/shard_map/ppermute | solution.py:15
  10.9 1.0 collective-permute-done
  11.9 0.9 scatter_custom_fusion
  12.9 0.8 scatter_custom_fusion.1
  13.7 3.5 %collective-permute-start.3 = (f32[7,1,1,1,768]{0,4,3,2,1:T(8,128)S(1)}, f32[7,1,1,1,768]{0,4,3,2,1:T(8,128)S(1)}, u32[]{:S(2)}, u32[]{:S(2)}) collective-permute-start(f32[7,1,1,1,768]{0,4,3,2,1:T(8,128)S(1)} %bitcast.97), channel_id=1, source_target_pairs={{4,0},{8,4},{12,8},{0,12},{5,1},{9,5},{13,9},{1,13},{6,2},{10,6},{... | collective-permute-start | bytes 64520 | tf_op jit(solution)/shard_map/ppermute | solution.py:27
  17.4 9.4 %collective-permute-done.3 = f32[7,1,1,1,768]{0,4,3,2,1:T(8,128)S(1)} collective-permute-done((f32[7,1,1,1,768]{0,4,3,2,1:T(8,128)S(1)}, f32[7,1,1,1,768]{0,4,3,2,1:T(8,128)S(1)}, u32[]{:S(2)}, u32[]{:S(2)}) %collective-permute-start.3) | collective-permute-done | bytes 21536 | tf_op jit(solution)/shard_map/ppermute | solution.py:27
  26.9 6.7 %collective-permute-done.2 = f32[7,1,1,1,768]{0,4,3,2,1:T(8,128)S(1)} collective-permute-done((f32[7,1,1,1,768]{0,4,3,2,1:T(8,128)S(1)}, f32[7,1,1,1,768]{0,4,3,2,1:T(8,128)S(1)}, u32[]{:S(2)}, u32[]{:S(2)}) %collective-permute-start.2) | collective-permute-done | bytes 21536 | tf_op jit(solution)/shard_map/ppermute | solution.py:24
  33.9 1.6 %collective-permute-start.5 = (f32[7,3,1,1,768]{4,3,2,1,0:T(1,128)S(1)}, f32[7,3,1,1,768]{4,3,2,1,0:T(1,128)S(1)}, u32[]{:S(2)}, u32[]{:S(2)}) collective-permute-start(f32[7,3,1,1,768]{4,3,2,1,0:T(1,128)S(1)} %pad_maximum_fusion.2), channel_id=1, source_target_pairs={{2,0},{0,2},{3,1},{1,3},{6,4},{4,6},{7,5},{5,7},{10,8},{8,10},{11,... | collective-permute-start | bytes 193544 | tf_op jit(solution)/shard_map/ppermute | solution.py:27
  36.0 2.2 %collective-permute-done.5 = f32[7,3,1,1,768]{4,3,2,1,0:T(1,128)S(1)} collective-permute-done((f32[7,3,1,1,768]{4,3,2,1,0:T(1,128)S(1)}, f32[7,3,1,1,768]{4,3,2,1,0:T(1,128)S(1)}, u32[]{:S(2)}, u32[]{:S(2)}) %collective-permute-start.5) | collective-permute-done | bytes 64544 | tf_op jit(solution)/shard_map/ppermute | solution.py:27
  38.2 1.5 collective-permute-done.4
  41.5 2.3 %fusion.34 = (f32[1,3,3,3,768]{4,0,3,2,1:T(1,128)S(1)}, f32[1,3,3,3,768]{4,0,3,2,1:T(1,128)S(1)}, f32[1,3,3,3,768]{4,0,3,2,1:T(1,128)S(1)}) fusion(f32[7,3,3,3,768]{4,0,3,2,1:T(8,128)S(1)} %copy_dynamic-update-slice_fusion.1, f32[3]{0:T(128)S(1)} %iota_add_fusion, f32[]{:T(128)} %bitcast.28, f32[]{:T(128)} %bitcast.32, f32[]{:T(128)} %bitcast.30), kind=kLoop, calls=%fused_computation.81 | loop fusion | flops 186624 | bytes 499212 | tf_op jit(solution)/shard_map/mul | solution.py:143
  44.2 72.7 %while.17 = (s32[]{:T(128)}, f32[6,3,128]{2,1,0:T(4,128)S(1)}, f32[6]{0:T(128)S(1)}, f32[6]{0:T(128)S(1)}, f32[]{:T(128)}, /*index=5*/s32[6]{0:T(128)S(1)}, f32[...) while((s32[]{:T(128)}, f32[6,3,128]{2,1,0:T(4,128)S(1)}, ...), condition=%wide.region_10.11_spmd, body=%wide.region_5.10_spmd.sunk | while | flops 20495192 | bytes 4781457 | solution.py:169
  50.5 3.8 %fusion.57 = (f32[]{:T(128)}, f32[]{:T(128)}, f32[16,128,128]{2,1,0:T(8,128)S(1)}) fusion(f32[128,128]{1,0:T(8,128)S(1)} %fusion.53, f32[16]{0:T(128)S(1)} %get-tuple-element.249, f32[16]{0:T(128)S(1)} %get-tuple-element.250, f32[16,128]{1,0:T(8,128)S(1)} %bitcast.104, f32[128]{0:T(128)S(1)} %get-tuple-element.253, f32[16,128]{1,0:T(8,128)S(1)} %bitcast.105, ...), kind=kLoop, calls=%fused_computation.33.clone.1 | loop fusion | flops 15990782 | bytes 2197644 | tf_op jit(solution)/shard_map/while/body/eval_jaxpr/reduce_sum | solution.py:78
  62.6 3.8 %fusion.57 = (f32[]{:T(128)}, f32[]{:T(128)}, f32[16,128,128]{2,1,0:T(8,128)S(1)}) fusion(f32[128,128]{1,0:T(8,128)S(1)} %fusion.53, f32[16]{0:T(128)S(1)} %get-tuple-element.249, f32[16]{0:T(128)S(1)} %get-tuple-element.250, f32[16,128]{1,0:T(8,128)S(1)} %bitcast.104, f32[128]{0:T(128)S(1)} %get-tuple-element.253, f32[16,128]{1,0:T(8,128)S(1)} %bitcast.105, ...), kind=kLoop, calls=%fused_computation.33.clone.1 | loop fusion | flops 15990782 | bytes 2197644 | tf_op jit(solution)/shard_map/while/body/eval_jaxpr/reduce_sum | solution.py:78
  66.9 0.8 dynamic_update_slice.25
  74.7 3.8 %fusion.57 = (f32[]{:T(128)}, f32[]{:T(128)}, f32[16,128,128]{2,1,0:T(8,128)S(1)}) fusion(f32[128,128]{1,0:T(8,128)S(1)} %fusion.53, f32[16]{0:T(128)S(1)} %get-tuple-element.249, f32[16]{0:T(128)S(1)} %get-tuple-element.250, f32[16,128]{1,0:T(8,128)S(1)} %bitcast.104, f32[128]{0:T(128)S(1)} %get-tuple-element.253, f32[16,128]{1,0:T(8,128)S(1)} %bitcast.105, ...), kind=kLoop, calls=%fused_computation.33.clone.1 | loop fusion | flops 15990782 | bytes 2197644 | tf_op jit(solution)/shard_map/while/body/eval_jaxpr/reduce_sum | solution.py:78
  86.8 3.8 %fusion.57 = (f32[]{:T(128)}, f32[]{:T(128)}, f32[16,128,128]{2,1,0:T(8,128)S(1)}) fusion(f32[128,128]{1,0:T(8,128)S(1)} %fusion.53, f32[16]{0:T(128)S(1)} %get-tuple-element.249, f32[16]{0:T(128)S(1)} %get-tuple-element.250, f32[16,128]{1,0:T(8,128)S(1)} %bitcast.104, f32[128]{0:T(128)S(1)} %get-tuple-element.253, f32[16,128]{1,0:T(8,128)S(1)} %bitcast.105, ...), kind=kLoop, calls=%fused_computation.33.clone.1 | loop fusion | flops 15990782 | bytes 2197644 | tf_op jit(solution)/shard_map/while/body/eval_jaxpr/reduce_sum | solution.py:78
  98.9 3.8 %fusion.57 = (f32[]{:T(128)}, f32[]{:T(128)}, f32[16,128,128]{2,1,0:T(8,128)S(1)}) fusion(f32[128,128]{1,0:T(8,128)S(1)} %fusion.53, f32[16]{0:T(128)S(1)} %get-tuple-element.249, f32[16]{0:T(128)S(1)} %get-tuple-element.250, f32[16,128]{1,0:T(8,128)S(1)} %bitcast.104, f32[128]{0:T(128)S(1)} %get-tuple-element.253, f32[16,128]{1,0:T(8,128)S(1)} %bitcast.105, ...), kind=kLoop, calls=%fused_computation.33.clone.1 | loop fusion | flops 15990782 | bytes 2197644 | tf_op jit(solution)/shard_map/while/body/eval_jaxpr/reduce_sum | solution.py:78
  103.2 0.8 dynamic_update_slice.25
  111.1 3.8 %fusion.57 = (f32[]{:T(128)}, f32[]{:T(128)}, f32[16,128,128]{2,1,0:T(8,128)S(1)}) fusion(f32[128,128]{1,0:T(8,128)S(1)} %fusion.53, f32[16]{0:T(128)S(1)} %get-tuple-element.249, f32[16]{0:T(128)S(1)} %get-tuple-element.250, f32[16,128]{1,0:T(8,128)S(1)} %bitcast.104, f32[128]{0:T(128)S(1)} %get-tuple-element.253, f32[16,128]{1,0:T(8,128)S(1)} %bitcast.105, ...), kind=kLoop, calls=%fused_computation.33.clone.1 | loop fusion | flops 15990782 | bytes 2197644 | tf_op jit(solution)/shard_map/while/body/eval_jaxpr/reduce_sum | solution.py:78
  115.4 0.8 dynamic_update_slice.25
  118.7 31.8 %all-reduce = (f32[]{:T(128)}, f32[]{:T(128)}) all-reduce(f32[]{:T(128)} %reduce_sum.96, f32[]{:T(128)} %reduce_sum.97), channel_id=1, replica_groups=mesh['win'=2,'dx'=4,'dy'=2,'dz'=2] {'dx','dy','dz'}, use_global_device_ids=true, to_apply=%region_12.13 | all-reduce | flops 2 | bytes 16 | tf_op jit(solution)/shard_map/psum | solution.py:171
  (151 shorter events, 36.6 us)
Async XLA Ops:
  0.6 12.2 %copy-start.2 = (f32[7]{0:T(128)S(1)}, f32[7]{0:T(128)}, u32[]{:S(2)}) copy-start(f32[7]{0:T(128)} %constant.159.clone.1) | copy-start | bytes 88
  5.1 6.8 %collective-permute-start = (f32[7,16]{0,1:T(8,128)S(1)}, f32[7,16]{0,1:T(8,128)S(1)}, u32[]{:S(2)}, u32[]{:S(2)}) collective-permute-start(f32[7,16]{0,1:T(8,128)S(1)} %bitcast.113), channel_id=1, source_target_pairs={{0,4},{4,8},{8,12},{12,0},{1,5},{5,9},{9,13},{13,1},{2,6},{6,10},{... | collective-permute-start | bytes 1352 | tf_op jit(solution)/shard_map/ppermute | solution.py:15
  8.8 27.1 %copy-start.1 = (s32[1,1,1,6,16]{4,2,3,1,0:T(1,128)S(1)}, s32[1,1,1,6,16]{4,2,3,1,0:T(1,128)}, u32[]{:S(2)}) copy-start(s32[1,1,1,6,16]{4,2,3,1,0:T(1,128)} %param.19) | copy-start | bytes 1156
  8.8 4.0 %collective-permute-start.1 = (f32[7,16]{0,1:T(8,128)S(1)}, f32[7,16]{0,1:T(8,128)S(1)}, u32[]{:S(2)}, u32[]{:S(2)}) collective-permute-start(f32[7,16]{0,1:T(8,128)S(1)} %bitcast.112), channel_id=1, source_target_pairs={{0,12},{4,0},{8,4},{12,8},{1,13},{5,1},{9,5},{13,9},{2,14},{6,2},{... | collective-permute-start | bytes 1352 | tf_op jit(solution)/shard_map/ppermute | solution.py:15
  12.8 27.1 %copy-start = (f32[3]{0:T(128)S(1)}, f32[3]{0:T(128)}, u32[]{:S(2)}) copy-start(f32[3]{0:T(128)} %param.24) | copy-start | bytes 40
  13.7 13.0 %collective-permute-start.3 = (f32[7,1,1,1,768]{0,4,3,2,1:T(8,128)S(1)}, f32[7,1,1,1,768]{0,4,3,2,1:T(8,128)S(1)}, u32[]{:S(2)}, u32[]{:S(2)}) collective-permute-start(f32[7,1,1,1,768]{0,4,3,2,1:T(8,128)S(1)} %bitcast.97), channel_id=1, source_target_pairs={{4,0},{8,4},{12,8},{0,12},{5,1},{9,5},{13,9},{1,13},{6,2},{10,6},{... | collective-permute-start | bytes 64520 | tf_op jit(solution)/shard_map/ppermute | solution.py:27
  17.2 16.4 %collective-permute-start.2 = (f32[7,1,1,1,768]{0,4,3,2,1:T(8,128)S(1)}, f32[7,1,1,1,768]{0,4,3,2,1:T(8,128)S(1)}, u32[]{:S(2)}, u32[]{:S(2)}) collective-permute-start(f32[7,1,1,1,768]{0,4,3,2,1:T(8,128)S(1)} %bitcast.98), channel_id=1, source_target_pairs={{0,4},{4,8},{8,12},{12,0},{1,5},{5,9},{9,13},{13,1},{2,6},{6,10},{... | collective-permute-start | bytes 64520 | tf_op jit(solution)/shard_map/ppermute | solution.py:24
  33.9 4.3 %collective-permute-start.5 = (f32[7,3,1,1,768]{4,3,2,1,0:T(1,128)S(1)}, f32[7,3,1,1,768]{4,3,2,1,0:T(1,128)S(1)}, u32[]{:S(2)}, u32[]{:S(2)}) collective-permute-start(f32[7,3,1,1,768]{4,3,2,1,0:T(1,128)S(1)} %pad_maximum_fusion.2), channel_id=1, source_target_pairs={{2,0},{0,2},{3,1},{1,3},{6,4},{4,6},{7,5},{5,7},{10,8},{8,10},{11,... | collective-permute-start | bytes 193544 | tf_op jit(solution)/shard_map/ppermute | solution.py:27
  35.4 4.3 %collective-permute-start.4 = (f32[7,3,1,1,768]{4,3,2,1,0:T(1,128)S(1)}, f32[7,3,1,1,768]{4,3,2,1,0:T(1,128)S(1)}, u32[]{:S(2)}, u32[]{:S(2)}) collective-permute-start(f32[7,3,1,1,768]{4,3,2,1,0:T(1,128)S(1)} %pad_maximum_fusion.2), channel_id=1, source_target_pairs={{0,2},{2,0},{1,3},{3,1},{4,6},{6,4},{5,7},{7,5},{8,10},{10,8},{9,1... | collective-permute-start | bytes 193544 | tf_op jit(solution)/shard_map/ppermute | solution.py:24
  39.8 1.5 collective-permute-start.6
  41.5 2.7 %copy-start.3 = (s32[1,1,1,6]{3,2,1,0:T(1,128)S(1)}, s32[1,1,1,6]{3,2,1,0:T(1,128)}, u32[]{:S(2)}) copy-start(s32[1,1,1,6]{3,2,1,0:T(1,128)} %param.20) | copy-start | bytes 76
where the time goes:
time: 155 us; the launch traced here: 154 us
  other arithmetic  41.6 us (27%)
  blocking collectives  31.8 us (21%)
  local copies, waits for them, and re-layouts  23.9 us (15%)
  waiting for transfers between devices  21.5 us (14%)
  loops' own time  20 us (13%)
  starting transfers between devices  10.9 us (7%)
  between operations  4.44 us (3%)
    psum x1, blocking collectives, on_device(): lax.psum((jnp.sum(energies), jnp.sum(dhdls)), ('dx', 'dy', 'dz'))  31.8 us
    reduce_sum x6, other arithmetic, pair_block(): jnp.sum(flagged * (-total_pair + weight * (grad_six * sigma_six * soft_al...  23.1 us
    another operation x1, loops' own time, on_device(): lax.map(one_block, jnp.arange(block_total, dtype=jnp.int32))  20 us
    ppermute x2, waiting for transfers between devices, extended(): lax.ppermute(lax.slice_in_dim(block, 0, width, axis=dim), axis, backward)  11.6 us
    dynamic_update_slice x18, local copies, waits for them, and re-layouts, on_device(): lax.map(one_block, jnp.arange(block_total, dtype=jnp.int32))  9.16 us
    ppermute x2, waiting for transfers between devices, extended(): lax.ppermute(lax.slice_in_dim(block, block.shape[dim] - width, None, axis...  8.23 us
    ppermute x2, starting transfers between devices, passed_along(): lax.ppermute(array, axis, [(i, (i + by) % devices) for i in range(devices)])  5.2 us
    ppermute x2, starting transfers between devices, extended(): lax.ppermute(lax.slice_in_dim(block, 0, width, axis=dim), axis, backward)  5.1 us
  transfers between devices with their start and end apart: 7, of which 6 were waited for; matrix products, arithmetic and copies ran while one was open for 2% of the time, Pallas kernels for 0%

commit v1 on v0

--- a/solution.py
+++ b/solution.py
@@ -168,7 +168,9 @@
 
     forces, energies, dhdls = lax.map(one_block, jnp.arange(block_total, dtype=jnp.int32))
     forces = forces.transpose(1, 0, 2).reshape(3, 1, 1, 1, atom_count)
-    window_energy, window_dhdl = lax.psum((jnp.sum(energies), jnp.sum(dhdls)), ("dx", "dy", "dz"))
+    window_energy, window_dhdl = lax.psum(
+        lax.psum((jnp.sum(energies), jnp.sum(dhdls)), "dx"), ("dy", "dz")
+    )
     slot_total = jnp.float32(
         atom_count * lax.axis_size("dx") * lax.axis_size("dy") * lax.axis_size("dz")
     )

time: 155 us -> 141 us (0.910)
  blocking collectives: 31.8 us -> 17.1 us
    psum x1 -> x2, blocking collectives: 31.8 us -> 17.1 us  [the longest x1 10.8 us: on_device(): lax.psum((jnp.sum(energies), jnp.sum(dhdls)), 'dx')]
where the time goes in v1:
time: 141 us; the launch traced here: 139 us
  other arithmetic  41.6 us (30%)
  local copies, waits for them, and re-layouts  23.9 us (17%)
  waiting for transfers between devices  21.5 us (15%)
  loops' own time  20 us (14%)
  blocking collectives  17.1 us (12%)
  starting transfers between devices  10.9 us (8%)
  between operations  4.44 us (3%)
    reduce_sum x6, other arithmetic, pair_block(): jnp.sum(flagged * (-total_pair + weight * (grad_six * sigma_six * soft_al...  23.1 us
    another operation x1, loops' own time, on_device(): lax.map(one_block, jnp.arange(block_total, dtype=jnp.int32))  20 us
    ppermute x2, waiting for transfers between devices, extended(): lax.ppermute(lax.slice_in_dim(block, 0, width, axis=dim), axis, backward)  11.6 us
    psum x1, blocking collectives, on_device(): lax.psum((jnp.sum(energies), jnp.sum(dhdls)), 'dx')  10.8 us
    dynamic_update_slice x18, local copies, waits for them, and re-layouts, on_device(): lax.map(one_block, jnp.arange(block_total, dtype=jnp.int32))  9.16 us
    ppermute x2, waiting for transfers between devices, extended(): lax.ppermute(lax.slice_in_dim(block, block.shape[dim] - width, None, axis...  8.23 us
    psum x1, blocking collectives, on_device(): lax.psum(lax.psum((jnp.sum(energies), jnp.sum(dhdls)), 'dx'), ('dy', 'dz'))  6.35 us
    ppermute x2, starting transfers between devices, passed_along(): lax.ppermute(array, axis, [(i, (i + by) % devices) for i in range(devices)])  5.2 us
  transfers between devices with their start and end apart: 7, of which 6 were waited for; matrix products, arithmetic and copies ran while one was open for 2% of the time, Pallas kernels for 0%

profile of v1, /device:TPU:0, one launch (start us, length us, event | category | flops | bytes accessed | tf_op | source)
XLA Modules:
  0.0 139.4 jit_solution(8250437965450649995)
XLA Ops:
  2.8 0.8 select_reduce_fusion
  5.1 3.1 %collective-permute-start = (f32[7,16]{0,1:T(8,128)S(1)}, f32[7,16]{0,1:T(8,128)S(1)}, u32[]{:S(2)}, u32[]{:S(2)}) collective-permute-start(f32[7,16]{0,1:T(8,128)S(1)} %bitcast.113), channel_id=1, source_target_pairs={{0,4},{4,8},{8,12},{12,0},{1,5},{5,9},{9,13},{13,1},{2,6},{6,10},{... | collective-permute-start | bytes 1352 | tf_op jit(solution)/shard_map/ppermute | solution.py:15
  8.8 2.1 %collective-permute-start.1 = (f32[7,16]{0,1:T(8,128)S(1)}, f32[7,16]{0,1:T(8,128)S(1)}, u32[]{:S(2)}, u32[]{:S(2)}) collective-permute-start(f32[7,16]{0,1:T(8,128)S(1)} %bitcast.112), channel_id=1, source_target_pairs={{0,12},{4,0},{8,4},{12,8},{1,13},{5,1},{9,5},{13,9},{2,14},{6,2},{... | collective-permute-start | bytes 1352 | tf_op jit(solution)/shard_map/ppermute | solution.py:15
  10.9 1.0 collective-permute-done
  11.9 0.9 scatter_custom_fusion
  12.9 0.8 scatter_custom_fusion.1
  13.7 3.5 %collective-permute-start.3 = (f32[7,1,1,1,768]{0,4,3,2,1:T(8,128)S(1)}, f32[7,1,1,1,768]{0,4,3,2,1:T(8,128)S(1)}, u32[]{:S(2)}, u32[]{:S(2)}) collective-permute-start(f32[7,1,1,1,768]{0,4,3,2,1:T(8,128)S(1)} %bitcast.97), channel_id=1, source_target_pairs={{4,0},{8,4},{12,8},{0,12},{5,1},{9,5},{13,9},{1,13},{6,2},{10,6},{... | collective-permute-start | bytes 64520 | tf_op jit(solution)/shard_map/ppermute | solution.py:27
  17.4 9.4 %collective-permute-done.3 = f32[7,1,1,1,768]{0,4,3,2,1:T(8,128)S(1)} collective-permute-done((f32[7,1,1,1,768]{0,4,3,2,1:T(8,128)S(1)}, f32[7,1,1,1,768]{0,4,3,2,1:T(8,128)S(1)}, u32[]{:S(2)}, u32[]{:S(2)}) %collective-permute-start.3) | collective-permute-done | bytes 21536 | tf_op jit(solution)/shard_map/ppermute | solution.py:27
  26.9 6.7 %collective-permute-done.2 = f32[7,1,1,1,768]{0,4,3,2,1:T(8,128)S(1)} collective-permute-done((f32[7,1,1,1,768]{0,4,3,2,1:T(8,128)S(1)}, f32[7,1,1,1,768]{0,4,3,2,1:T(8,128)S(1)}, u32[]{:S(2)}, u32[]{:S(2)}) %collective-permute-start.2) | collective-permute-done | bytes 21536 | tf_op jit(solution)/shard_map/ppermute | solution.py:24
  33.9 1.6 %collective-permute-start.5 = (f32[7,3,1,1,768]{4,3,2,1,0:T(1,128)S(1)}, f32[7,3,1,1,768]{4,3,2,1,0:T(1,128)S(1)}, u32[]{:S(2)}, u32[]{:S(2)}) collective-permute-start(f32[7,3,1,1,768]{4,3,2,1,0:T(1,128)S(1)} %pad_maximum_fusion.2), channel_id=1, source_target_pairs={{2,0},{0,2},{3,1},{1,3},{6,4},{4,6},{7,5},{5,7},{10,8},{8,10},{11,... | collective-permute-start | bytes 193544 | tf_op jit(solution)/shard_map/ppermute | solution.py:27
  36.0 2.2 %collective-permute-done.5 = f32[7,3,1,1,768]{4,3,2,1,0:T(1,128)S(1)} collective-permute-done((f32[7,3,1,1,768]{4,3,2,1,0:T(1,128)S(1)}, f32[7,3,1,1,768]{4,3,2,1,0:T(1,128)S(1)}, u32[]{:S(2)}, u32[]{:S(2)}) %collective-permute-start.5) | collective-permute-done | bytes 64544 | tf_op jit(solution)/shard_map/ppermute | solution.py:27
  38.2 1.5 %collective-permute-done.4 = f32[7,3,1,1,768]{4,3,2,1,0:T(1,128)S(1)} collective-permute-done((f32[7,3,1,1,768]{4,3,2,1,0:T(1,128)S(1)}, f32[7,3,1,1,768]{4,3,2,1,0:T(1,128)S(1)}, u32[]{:S(2)}, u32[]{:S(2)}) %collective-permute-start.4) | collective-permute-done | bytes 64544 | tf_op jit(solution)/shard_map/ppermute | solution.py:24
  41.5 2.3 %fusion.34 = (f32[1,3,3,3,768]{4,0,3,2,1:T(1,128)S(1)}, f32[1,3,3,3,768]{4,0,3,2,1:T(1,128)S(1)}, f32[1,3,3,3,768]{4,0,3,2,1:T(1,128)S(1)}) fusion(f32[7,3,3,3,768]{4,0,3,2,1:T(8,128)S(1)} %copy_dynamic-update-slice_fusion.1, f32[3]{0:T(128)S(1)} %iota_add_fusion, f32[]{:T(128)} %bitcast.28, f32[]{:T(128)} %bitcast.32, f32[]{:T(128)} %bitcast.30), kind=kLoop, calls=%fused_computation.81 | loop fusion | flops 186624 | bytes 499212 | tf_op jit(solution)/shard_map/mul | solution.py:143
  44.2 72.7 %while.17 = (s32[]{:T(128)}, f32[6,3,128]{2,1,0:T(4,128)S(1)}, f32[6]{0:T(128)S(1)}, f32[6]{0:T(128)S(1)}, f32[]{:T(128)}, /*index=5*/s32[6]{0:T(128)S(1)}, f32[...) while((s32[]{:T(128)}, f32[6,3,128]{2,1,0:T(4,128)S(1)}, ...), condition=%wide.region_10.11_spmd, body=%wide.region_5.10_spmd.sunk | while | flops 20495192 | bytes 4781457 | solution.py:169
  50.5 3.8 %fusion.57 = (f32[]{:T(128)}, f32[]{:T(128)}, f32[16,128,128]{2,1,0:T(8,128)S(1)}) fusion(f32[128,128]{1,0:T(8,128)S(1)} %fusion.53, f32[16]{0:T(128)S(1)} %get-tuple-element.251, f32[16]{0:T(128)S(1)} %get-tuple-element.252, f32[16,128]{1,0:T(8,128)S(1)} %bitcast.104, f32[128]{0:T(128)S(1)} %get-tuple-element.255, f32[16,128]{1,0:T(8,128)S(1)} %bitcast.105, ...), kind=kLoop, calls=%fused_computation.33.clone.1 | loop fusion | flops 15990782 | bytes 2197644 | tf_op jit(solution)/shard_map/while/body/eval_jaxpr/reduce_sum | solution.py:78
  62.6 3.8 %fusion.57 = (f32[]{:T(128)}, f32[]{:T(128)}, f32[16,128,128]{2,1,0:T(8,128)S(1)}) fusion(f32[128,128]{1,0:T(8,128)S(1)} %fusion.53, f32[16]{0:T(128)S(1)} %get-tuple-element.251, f32[16]{0:T(128)S(1)} %get-tuple-element.252, f32[16,128]{1,0:T(8,128)S(1)} %bitcast.104, f32[128]{0:T(128)S(1)} %get-tuple-element.255, f32[16,128]{1,0:T(8,128)S(1)} %bitcast.105, ...), kind=kLoop, calls=%fused_computation.33.clone.1 | loop fusion | flops 15990782 | bytes 2197644 | tf_op jit(solution)/shard_map/while/body/eval_jaxpr/reduce_sum | solution.py:78
  66.9 0.8 dynamic_update_slice.25
  74.7 3.8 %fusion.57 = (f32[]{:T(128)}, f32[]{:T(128)}, f32[16,128,128]{2,1,0:T(8,128)S(1)}) fusion(f32[128,128]{1,0:T(8,128)S(1)} %fusion.53, f32[16]{0:T(128)S(1)} %get-tuple-element.251, f32[16]{0:T(128)S(1)} %get-tuple-element.252, f32[16,128]{1,0:T(8,128)S(1)} %bitcast.104, f32[128]{0:T(128)S(1)} %get-tuple-element.255, f32[16,128]{1,0:T(8,128)S(1)} %bitcast.105, ...), kind=kLoop, calls=%fused_computation.33.clone.1 | loop fusion | flops 15990782 | bytes 2197644 | tf_op jit(solution)/shard_map/while/body/eval_jaxpr/reduce_sum | solution.py:78
  86.8 3.8 %fusion.57 = (f32[]{:T(128)}, f32[]{:T(128)}, f32[16,128,128]{2,1,0:T(8,128)S(1)}) fusion(f32[128,128]{1,0:T(8,128)S(1)} %fusion.53, f32[16]{0:T(128)S(1)} %get-tuple-element.251, f32[16]{0:T(128)S(1)} %get-tuple-element.252, f32[16,128]{1,0:T(8,128)S(1)} %bitcast.104, f32[128]{0:T(128)S(1)} %get-tuple-element.255, f32[16,128]{1,0:T(8,128)S(1)} %bitcast.105, ...), kind=kLoop, calls=%fused_computation.33.clone.1 | loop fusion | flops 15990782 | bytes 2197644 | tf_op jit(solution)/shard_map/while/body/eval_jaxpr/reduce_sum | solution.py:78
  98.9 3.8 %fusion.57 = (f32[]{:T(128)}, f32[]{:T(128)}, f32[16,128,128]{2,1,0:T(8,128)S(1)}) fusion(f32[128,128]{1,0:T(8,128)S(1)} %fusion.53, f32[16]{0:T(128)S(1)} %get-tuple-element.251, f32[16]{0:T(128)S(1)} %get-tuple-element.252, f32[16,128]{1,0:T(8,128)S(1)} %bitcast.104, f32[128]{0:T(128)S(1)} %get-tuple-element.255, f32[16,128]{1,0:T(8,128)S(1)} %bitcast.105, ...), kind=kLoop, calls=%fused_computation.33.clone.1 | loop fusion | flops 15990782 | bytes 2197644 | tf_op jit(solution)/shard_map/while/body/eval_jaxpr/reduce_sum | solution.py:78
  103.2 0.8 dynamic_update_slice.25
  111.1 3.8 %fusion.57 = (f32[]{:T(128)}, f32[]{:T(128)}, f32[16,128,128]{2,1,0:T(8,128)S(1)}) fusion(f32[128,128]{1,0:T(8,128)S(1)} %fusion.53, f32[16]{0:T(128)S(1)} %get-tuple-element.251, f32[16]{0:T(128)S(1)} %get-tuple-element.252, f32[16,128]{1,0:T(8,128)S(1)} %bitcast.104, f32[128]{0:T(128)S(1)} %get-tuple-element.255, f32[16,128]{1,0:T(8,128)S(1)} %bitcast.105, ...), kind=kLoop, calls=%fused_computation.33.clone.1 | loop fusion | flops 15990782 | bytes 2197644 | tf_op jit(solution)/shard_map/while/body/eval_jaxpr/reduce_sum | solution.py:78
  118.7 10.8 %all-reduce.1 = (f32[]{:T(128)}, f32[]{:T(128)}) all-reduce(f32[]{:T(128)} %reduce_sum.96, f32[]{:T(128)} %reduce_sum.97), channel_id=1, replica_groups=mesh['win'=2,'dx'=4,'dy'=2,'dz'=2] {'dx'}, use_global_device_ids=true, to_apply=%region_12.13 | all-reduce | flops 2 | bytes 16 | tf_op jit(solution)/shard_map/psum | solution.py:172
  129.5 6.3 %all-reduce = (f32[]{:T(128)}, f32[]{:T(128)}) all-reduce(f32[]{:T(128)} %get-tuple-element.158, f32[]{:T(128)} %get-tuple-element.159), channel_id=1, replica_groups=mesh['win'=2,'dx'=4,'dy'=2,'dz'=2] {'dy','dz'}, use_global_device_ids=true, to_apply=%region_13.14 | all-reduce | flops 2 | bytes 16 | tf_op jit(solution)/shard_map/psum | solution.py:171
  (152 shorter events, 37.3 us)
Async XLA Ops:
  0.6 12.2 %copy-start.2 = (f32[7]{0:T(128)S(1)}, f32[7]{0:T(128)}, u32[]{:S(2)}) copy-start(f32[7]{0:T(128)} %constant.159.clone.1) | copy-start | bytes 88
  5.1 6.8 %collective-permute-start = (f32[7,16]{0,1:T(8,128)S(1)}, f32[7,16]{0,1:T(8,128)S(1)}, u32[]{:S(2)}, u32[]{:S(2)}) collective-permute-start(f32[7,16]{0,1:T(8,128)S(1)} %bitcast.113), channel_id=1, source_target_pairs={{0,4},{4,8},{8,12},{12,0},{1,5},{5,9},{9,13},{13,1},{2,6},{6,10},{... | collective-permute-start | bytes 1352 | tf_op jit(solution)/shard_map/ppermute | solution.py:15
  8.8 27.1 %copy-start.1 = (s32[1,1,1,6,16]{4,2,3,1,0:T(1,128)S(1)}, s32[1,1,1,6,16]{4,2,3,1,0:T(1,128)}, u32[]{:S(2)}) copy-start(s32[1,1,1,6,16]{4,2,3,1,0:T(1,128)} %param.19) | copy-start | bytes 1156
  8.8 4.0 %collective-permute-start.1 = (f32[7,16]{0,1:T(8,128)S(1)}, f32[7,16]{0,1:T(8,128)S(1)}, u32[]{:S(2)}, u32[]{:S(2)}) collective-permute-start(f32[7,16]{0,1:T(8,128)S(1)} %bitcast.112), channel_id=1, source_target_pairs={{0,12},{4,0},{8,4},{12,8},{1,13},{5,1},{9,5},{13,9},{2,14},{6,2},{... | collective-permute-start | bytes 1352 | tf_op jit(solution)/shard_map/ppermute | solution.py:15
  12.8 27.1 %copy-start = (f32[3]{0:T(128)S(1)}, f32[3]{0:T(128)}, u32[]{:S(2)}) copy-start(f32[3]{0:T(128)} %param.24) | copy-start | bytes 40
  13.7 13.0 %collective-permute-start.3 = (f32[7,1,1,1,768]{0,4,3,2,1:T(8,128)S(1)}, f32[7,1,1,1,768]{0,4,3,2,1:T(8,128)S(1)}, u32[]{:S(2)}, u32[]{:S(2)}) collective-permute-start(f32[7,1,1,1,768]{0,4,3,2,1:T(8,128)S(1)} %bitcast.97), channel_id=1, source_target_pairs={{4,0},{8,4},{12,8},{0,12},{5,1},{9,5},{13,9},{1,13},{6,2},{10,6},{... | collective-permute-start | bytes 64520 | tf_op jit(solution)/shard_map/ppermute | solution.py:27
  17.2 16.4 %collective-permute-start.2 = (f32[7,1,1,1,768]{0,4,3,2,1:T(8,128)S(1)}, f32[7,1,1,1,768]{0,4,3,2,1:T(8,128)S(1)}, u32[]{:S(2)}, u32[]{:S(2)}) collective-permute-start(f32[7,1,1,1,768]{0,4,3,2,1:T(8,128)S(1)} %bitcast.98), channel_id=1, source_target_pairs={{0,4},{4,8},{8,12},{12,0},{1,5},{5,9},{9,13},{13,1},{2,6},{6,10},{... | collective-permute-start | bytes 64520 | tf_op jit(solution)/shard_map/ppermute | solution.py:24
  33.9 4.3 %collective-permute-start.5 = (f32[7,3,1,1,768]{4,3,2,1,0:T(1,128)S(1)}, f32[7,3,1,1,768]{4,3,2,1,0:T(1,128)S(1)}, u32[]{:S(2)}, u32[]{:S(2)}) collective-permute-start(f32[7,3,1,1,768]{4,3,2,1,0:T(1,128)S(1)} %pad_maximum_fusion.2), channel_id=1, source_target_pairs={{2,0},{0,2},{3,1},{1,3},{6,4},{4,6},{7,5},{5,7},{10,8},{8,10},{11,... | collective-permute-start | bytes 193544 | tf_op jit(solution)/shard_map/ppermute | solution.py:27
  35.4 4.3 %collective-permute-start.4 = (f32[7,3,1,1,768]{4,3,2,1,0:T(1,128)S(1)}, f32[7,3,1,1,768]{4,3,2,1,0:T(1,128)S(1)}, u32[]{:S(2)}, u32[]{:S(2)}) collective-permute-start(f32[7,3,1,1,768]{4,3,2,1,0:T(1,128)S(1)} %pad_maximum_fusion.2), channel_id=1, source_target_pairs={{0,2},{2,0},{1,3},{3,1},{4,6},{6,4},{5,7},{7,5},{8,10},{10,8},{9,1... | collective-permute-start | bytes 193544 | tf_op jit(solution)/shard_map/ppermute | solution.py:24
  39.8 1.5 %collective-permute-start.6 = (f32[7,3,3,1,768]{4,3,2,1,0:T(1,128)S(1)}, f32[7,3,3,1,768]{4,3,2,1,0:T(1,128)S(1)}, u32[]{:S(2)}, u32[]{:S(2)}) collective-permute-start(f32[7,3,3,1,768]{4,3,2,1,0:T(1,128)S(1)} %pad_maximum_fusion.1), channel_id=1, source_target_pairs={{0,1},{1,0},{2,3},{3,2},{4,5},{5,4},{6,7},{7,6},{8,9},{9,8},{10,11... | collective-permute-start | bytes 580616 | tf_op jit(solution)/shard_map/ppermute | solution.py:39
  41.5 2.7 %copy-start.3 = (s32[1,1,1,6]{3,2,1,0:T(1,128)S(1)}, s32[1,1,1,6]{3,2,1,0:T(1,128)}, u32[]{:S(2)}) copy-start(s32[1,1,1,6]{3,2,1,0:T(1,128)} %param.20) | copy-start | bytes 76
